TPU v7x, 256 devices: a whole 4x4x8 slice. The times are simulated.
256 devices in a mesh: dp: 64 (over y, z, core), mp: 4 (over x).
Axes of the slice: x: 4, y: 4, z: 8, core: 2. Of those that a mesh axis runs over, the one named last changes fastest.
Arguments:
- queries: bfloat16 [196608, 2048], P('dp', 'mp'), may hold values from -30 to 30
- keys: bfloat16 [196608, 512], P('dp', 'mp'), may hold values from -30 to 30
- values: bfloat16 [196608, 512], P('dp', 'mp'), may hold values from -6 to 6
- doc_ids: int32 [196608], P('dp'), may hold values from -1 to 127, as said below
- live_counts: int32 [64], P('dp'), may hold values from 1 to 24, 1408 in all
- out_weight: bfloat16 [2048, 4096], P('dp', 'mp'), may hold values from -0.125 to 0.125
Outputs:
- mixed: bfloat16 [180224, 4096], P('dp', 'mp')
Inputs may be any that keep to these rules, and one draw needn't show every extreme that they name: `live_counts`: each device has 1 to 24 live blocks, 1408 in all, and some device has exactly 24. `doc_ids`: within each block the numbers start at 0 and never fall along the block, and the -1 entries, if any, form the block's tail.
All inputs are finite; a program needn't handle non-finite values.
Results may differ from a plain program's by a relative error of at most 0.0049.
Values may be sent and summed in bfloat16 or wider, within the bound.
No kernel may reach another device: no remote copies, remote signals or barrier semaphores. Data moves between devices by JAX's collectives and lax.ppermute only.
A program may use at most 128 MiB of HBM per device.

v0:
```python
import math
import jax
import jax.numpy as jnp
from jax import lax
from jax.sharding import PartitionSpec as P

HEAD_SIZE = 128
BLOCK = 128
NB = 24
masked_score = -1e30


def from_everyone(shard, axis):
    size = lax.axis_size(axis)
    return lax.all_to_all(
        jnp.broadcast_to(shard[None], (size, *shard.shape)), axis, 0, 0, tiled=True
    )


def in_order(pieces, dim):
    shape = list(pieces.shape[1:])
    shape[dim] *= pieces.shape[0]
    return jnp.moveaxis(pieces, 0, dim).reshape(shape)


def gather_directly(shard, axis, dim):
    pieces = from_everyone(shard, axis)
    return in_order(pieces, dim)


def group_size():
    return 4


def attend_group(operands):
    query_blocks, key_blocks, value_blocks, id_blocks = operands
    number = query_blocks.shape[0]
    query_heads = query_blocks.shape[2] // HEAD_SIZE
    key_heads = key_blocks.shape[2] // HEAD_SIZE
    repeat = query_heads // key_heads
    query_four = query_blocks.reshape(number, BLOCK, key_heads, repeat, HEAD_SIZE)
    key_four = key_blocks.reshape(number, BLOCK, key_heads, HEAD_SIZE)
    value_four = value_blocks.reshape(number, BLOCK, key_heads, HEAD_SIZE)
    scores = jnp.einsum(
        "bihrd,bjhd->bhrij", query_four, key_four, preferred_element_type=jnp.float32
    ) / math.sqrt(HEAD_SIZE)
    places = jnp.arange(BLOCK, dtype=jnp.int32)
    causal = places[None, :] <= places[:, None]
    allowed = (id_blocks[:, :, None] == id_blocks[:, None, :]) & causal[None]
    scores = jnp.where(allowed[:, None, None], scores, masked_score)
    highest = jnp.max(scores, axis=-1, keepdims=True)
    weights = jnp.where(allowed[:, None, None], jnp.exp(scores - highest), 0.0)
    total_counts = jnp.sum(weights, axis=-1)
    summed = jnp.einsum(
        "bhrij,bjhd->bihrd",
        weights.astype(jnp.bfloat16),
        value_four,
        preferred_element_type=jnp.float32,
    )
    summed = summed / jnp.transpose(total_counts, (0, 3, 1, 2))[..., None]
    summed = jnp.where(id_blocks[:, :, None, None, None] >= 0, summed, 0.0)
    return summed.reshape(number, BLOCK, query_heads * HEAD_SIZE).astype(jnp.bfloat16)


def attend_blocks(query_blocks, key_blocks, value_blocks, id_blocks):
    number = query_blocks.shape[0]
    grouping = group_size()

    def regroup(tensor):
        return tensor.reshape((number // grouping, grouping) + tensor.shape[1:])

    result = lax.map(
        attend_group,
        (regroup(query_blocks), regroup(key_blocks), regroup(value_blocks), regroup(id_blocks)),
    )
    return result.reshape((number,) + result.shape[2:])


def locate(labels, targets):
    slots = jnp.arange(labels.shape[0], dtype=jnp.int32)
    hits = labels[None, :] == targets[:, None]
    return jnp.sum(jnp.where(hits, slots[None, :], 0), axis=1)


def body(queries, keys, values, doc_ids, live_counts, out_weight):
    member_list = lax.axis_size("dp")
    per_owner = (NB + member_list - 1) // member_list
    kept_blocks = NB * 11 // 12
    own_index = lax.axis_index("dp")
    live_blocks = live_counts[0]
    full_weight = lax.all_gather(out_weight, "dp", axis=0, tiled=True)
    table = gather_directly(live_counts, "dp", 0)
    first_label = jnp.sum(jnp.where(jnp.arange(member_list, dtype=jnp.int32) < own_index, table, 0))
    owners = jnp.arange(member_list, dtype=jnp.int32)[:, None]
    layers = jnp.arange(per_owner, dtype=jnp.int32)[None, :]
    chosen = ((owners - first_label) % member_list + layers * member_list).reshape(-1)
    usable = chosen < live_blocks
    labels = jnp.where(usable, first_label + chosen, -1)
    chosen = jnp.where(usable, chosen, 0)
    query_cols = queries.shape[1]
    query_blocks = queries.reshape(NB, BLOCK, query_cols)
    key_blocks = keys.reshape(NB, BLOCK, keys.shape[1])
    value_blocks = values.reshape(NB, BLOCK, values.shape[1])
    id_blocks = doc_ids.reshape(NB, BLOCK)
    targets = own_index + jnp.arange(kept_blocks, dtype=jnp.int32) * member_list
    own_result = attend_blocks(query_blocks, key_blocks, value_blocks, id_blocks)
    arrived = (
        lax.all_to_all(own_result[chosen], "dp", split_axis=0, concat_axis=0, tiled=True),
        lax.all_to_all(labels, "dp", split_axis=0, concat_axis=0, tiled=True),
    )
    source = locate(arrived[1], targets)
    attended = arrived[0][source]
    flattened = attended.reshape(kept_blocks * BLOCK, query_cols)
    mixed = jnp.dot(
        lax.all_gather(flattened, "mp", axis=1, tiled=True),
        full_weight,
        preferred_element_type=jnp.float32,
    )
    return mixed.astype(jnp.bfloat16)


def solution(mesh):
    return jax.shard_map(
        body,
        mesh=mesh,
        in_specs=(P("dp", "mp"), P("dp", "mp"), P("dp", "mp"), P("dp"), P("dp"), P("dp", "mp")),
        out_specs=P("dp", "mp"),
        check_vma=False,
    )
```

profile of v0, /device:TPU:1, one launch (start us, length us, event | category | flops | bytes accessed | tf_op | source)
XLA Modules:
  0.0 426.4 jit_solution(5800160574564493758)
XLA Ops:
  7.2 0.6 broadcast_in_dim.83
  7.8 13.1 %all-to-all-start = ((s32[64,1,1]{2,1,0:T(1,128)}), s32[64,1,1]{2,1,0:T(1,128)S(1)}, u32[]{:S(2)}, u32[]{:S(2)}) async-start(s32[64,1,1]{2,1,0:T(1,128)} %broadcast_in_dim.83), calls=%async_computation | async-start | bytes 65536 | tf_op jit(solution)/shard_map/all_to_all | solution.py:15
  21.0 35.9 %while.10 = (s32[]{:T(128)}, bf16[6,4,128,512]{3,2,1,0:T(8,128)(2,1)}, s32[6,4,128]{2,1,0:T(4,128)}, bf16[6,4,128,128]{3,2,1,0:T(8,128)(2,1)}, bf16[6,4,128,128]...) while((s32[]{:T(128)}, bf16[6,4,128,512]{3,2,1,0:T(8,128)(2,1)}, s32[6,4,128]{2,1,0:T(4,128)}, ...), condition=%wide.region_3.4_spmd, body=%wide.region_0.3_spmd.sunk | while | flops 137507328 | bytes 8993897 | solution.py:72
  21.0 0.7 broadcast_compare_fusion.2
  21.8 1.1 constant_dynamic-slice_fusion.2
  22.9 0.3 copy.45
  23.2 1.2 fusion.33
  24.7 1.3 select_convert_fusion.2
  26.1 0.8 constant_dynamic-update-slice_fusion.2
  27.0 0.7 broadcast_compare_fusion.2
  27.8 1.1 constant_dynamic-slice_fusion.2
  29.2 1.2 fusion.33
  30.6 1.3 select_convert_fusion.2
  32.1 0.8 constant_dynamic-update-slice_fusion.2
  33.0 0.7 broadcast_compare_fusion.2
  33.8 1.1 constant_dynamic-slice_fusion.2
  35.2 1.2 fusion.33
  36.6 1.3 select_convert_fusion.2
  38.1 0.8 constant_dynamic-update-slice_fusion.2
  38.9 0.7 broadcast_compare_fusion.2
  39.8 1.1 constant_dynamic-slice_fusion.2
  41.2 1.2 fusion.33
  42.6 1.3 select_convert_fusion.2
  44.1 0.8 constant_dynamic-update-slice_fusion.2
  44.9 0.7 broadcast_compare_fusion.2
  45.8 1.1 constant_dynamic-slice_fusion.2
  47.2 1.2 fusion.33
  48.6 1.3 select_convert_fusion.2
  50.1 0.8 constant_dynamic-update-slice_fusion.2
  50.9 0.7 broadcast_compare_fusion.2
  51.8 1.1 constant_dynamic-slice_fusion.2
  53.1 1.2 fusion.33
  54.6 1.3 select_convert_fusion.2
  56.1 0.8 constant_dynamic-update-slice_fusion.2
  56.9 1.2 reduce.2
  58.1 0.7 fusion.17
  58.9 0.7 fusion.19
  59.6 1.4 compare_select_fusion.2
  61.0 10.3 %all-to-all-start.2 = ((s32[64,1,1]{2,1,0:T(1,128)}), s32[64,1,1]{2,1,0:T(1,128)S(1)}, u32[]{:S(2)}, u32[]{:S(2)}) async-start(s32[64,1,1]{2,1,0:T(1,128)} %compare_select_fusion.2), calls=%async_computation.2 | async-start | bytes 65536 | tf_op jit(solution)/shard_map/all_to_all | solution.py:109
  71.3 7.3 %gather_fusion = bf16[64,128,512]{2,1,0:T(8,128)(2,1)} fusion(bf16[24,128,512]{2,1,0:T(8,128)(2,1)} %bitcast.76, s32[1024]{0:T(1024)S(1)} %pad_clamp_fusion.1), kind=kCustom, calls=%fused_computation | custom fusion | bytes 16777472 | tf_op jit(solution)/shard_map/gather | solution.py:108
  78.7 2.0 all-to-all-done.2
  80.6 8.5 %all-to-all-start.1 = ((bf16[64,128,512]{2,1,0:T(8,128)(2,1)}), bf16[64,128,512]{2,1,0:T(8,128)(2,1)}, u32[]{:S(2)}, u32[]{:S(2)}) async-start(bf16[64,128,512]{2,1,0:T(8,128)(2,1)} %gather_fusion), calls=%async_computation.1 | async-start | bytes 16777216 | tf_op jit(solution)/shard_map/all_to_all | solution.py:108
  89.1 0.7 all-gather.5.cloned.1.call-update
  90.1 1.2 reduce.3
  91.5 195.6 %all-to-all-done.1 = bf16[64,128,512]{2,1,0:T(8,128)(2,1)} async-done(((bf16[64,128,512]{2,1,0:T(8,128)(2,1)}), bf16[64,128,512]{2,1,0:T(8,128)(2,1)}, u32[]{:S(2)}, u32[]{:S(2)}) %all-to-all-start.1) | async-done | bytes 8388640 | tf_op jit(solution)/shard_map/all_to_all | solution.py:108
  287.1 5.8 %gather_fusion.1 = bf16[22,128,512]{2,1,0:T(8,128)(2,1)} fusion(bf16[64,128,512]{2,1,0:T(8,128)(2,1)} %all-to-all-done.1, s32[1024]{0:T(1024)S(1)} %pad_clamp_fusion), kind=kCustom, calls=%fused_computation.1 | custom fusion | bytes 5767256 | tf_op jit(solution)/shard_map/gather | solution.py:112
  293.0 108.8 %all-gather.3.cloned.1.call-done = bf16[2816,2048]{1,0:T(8,128)(2,1)} async-done(((bf16[2816,512]{1,0:T(8,128)(2,1)}), bf16[2816,2048]{1,0:T(8,128)(2,1)}) %all-gather.3.cloned.1.call-update) | async-done | bytes 11534352 | tf_op jit(solution)/shard_map/all_gather | solution.py:115
  401.8 17.8 %convolution_convert_fusion = bf16[2816,1024]{1,0:T(8,128)(2,1)} fusion(bf16[2816,2048]{1,0:T(8,128)(2,1)} %all-gather.3.cloned.1.call-done, bf16[2048,1024]{1,0:T(8,128)(2,1)} %all-gather.5.cloned.1.call-done), kind=kOutput, calls=%fused_computation.27 | convolution fusion | flops 11814043648 | bytes 21495808 | tf_op jit(solution)/shard_map/dot_general | solution.py:114
  (40 shorter events, 5.5 us)
Async XLA Ops:
  7.8 49.1 %all-to-all-start = ((s32[64,1,1]{2,1,0:T(1,128)}), s32[64,1,1]{2,1,0:T(1,128)S(1)}, u32[]{:S(2)}, u32[]{:S(2)}) async-start(s32[64,1,1]{2,1,0:T(1,128)} %broadcast_in_dim.83), calls=%async_computation | async-start | bytes 65536 | tf_op jit(solution)/shard_map/all_to_all | solution.py:15
  61.0 19.6 %all-to-all-start.2 = ((s32[64,1,1]{2,1,0:T(1,128)}), s32[64,1,1]{2,1,0:T(1,128)S(1)}, u32[]{:S(2)}, u32[]{:S(2)}) async-start(s32[64,1,1]{2,1,0:T(1,128)} %compare_select_fusion.2), calls=%async_computation.2 | async-start | bytes 65536 | tf_op jit(solution)/shard_map/all_to_all | solution.py:109
  80.6 206.5 %all-to-all-start.1 = ((bf16[64,128,512]{2,1,0:T(8,128)(2,1)}), bf16[64,128,512]{2,1,0:T(8,128)(2,1)}, u32[]{:S(2)}, u32[]{:S(2)}) async-start(bf16[64,128,512]{2,1,0:T(8,128)(2,1)} %gather_fusion), calls=%async_computation.1 | async-start | bytes 16777216 | tf_op jit(solution)/shard_map/all_to_all | solution.py:108
  89.1 203.9 %all-gather.5.cloned.1.call-start = ((), (), s32[]{:S(2)}) async-start(), calls=%async_computation.4 | async-start | bytes 4259840 | tf_op jit(solution)/shard_map/all_gather | solution.py:91
  89.8 311.9 %all-gather.3.cloned.1.call-start = ((), (), s32[]{:S(2)}) async-start(), calls=%async_computation.3 | async-start | bytes 14417920 | tf_op jit(solution)/shard_map/all_gather | solution.py:115
Sparse Core Ops, SparseCore 0:
  92.7 101.4 all-gather.4
  293.1 108.6 all-gather.2
where the time goes:
time: 427 us; the launch traced here: 426 us
  waiting for transfers between devices  307 us (72%)
  matrix products  32.6 us (8%)
  starting transfers between devices  32.2 us (8%)
  local copies, waits for them, and re-layouts  28.3 us (7%)
  between operations  14.1 us (3%)
  other arithmetic  11.8 us (3%)
    all_to_all x1, waiting for transfers between devices, body(): lax.all_to_all(own_result[chosen], 'dp', split_axis=0, concat_axis=0, til...  196 us
    all_gather x1, waiting for transfers between devices, body(): lax.all_gather(flattened, 'mp', axis=1, tiled=True)  109 us
    dot_general x1, matrix products, body(): jnp.dot(lax.all_gather(flattened, 'mp', axis=1, tiled=True), full_weight,...  17.8 us
    all_to_all x1, starting transfers between devices, from_everyone(): lax.all_to_all(jnp.broadcast_to(shard[None], (size, *shard.shape)), axis,...  13.1 us
    all_to_all x1, starting transfers between devices, body(): lax.all_to_all(labels, 'dp', split_axis=0, concat_axis=0, tiled=True)  10.3 us
  transfers between devices with their start and end apart: 5, of which 3 were waited for; matrix products, arithmetic and copies ran while one was open for 12% of the time, Pallas kernels for 0%

commit v1 on v0

--- a/solution.py
+++ b/solution.py
@@ -112,7 +112,9 @@
     attended = arrived[0][source]
     flattened = attended.reshape(kept_blocks * BLOCK, query_cols)
     mixed = jnp.dot(
-        lax.all_gather(flattened, "mp", axis=1, tiled=True),
+        jnp.concatenate(
+            lax.all_to_all(jnp.stack([flattened] * lax.axis_size("mp")), "mp", 0, 0), axis=1
+        ),
         full_weight,
         preferred_element_type=jnp.float32,
     )

time: 427 us -> 449 us (1.052)
  local copies, waits for them, and re-layouts: 28.3 us -> 36.2 us
  starting transfers between devices: 32.2 us -> 39 us
  waiting for transfers between devices: 307 us -> 313 us
    all_gather x1 -> x0, waiting for transfers between devices: 109 us -> none  [body(): lax.all_gather(flattened, 'mp', axis=1, tiled=True)]
    all_gather x1, waiting for transfers between devices: 0.02 us -> 79.1 us  [body(): full_weight = lax.all_gather(out_weight, 'dp', axis=0, tiled=True)]
    all_to_all x0 -> x1, waiting for transfers between devices: none -> 48.2 us  [body(): lax.all_to_all(jnp.stack([flattened] * lax.axis_size('mp')), 'mp', 0, 0)]
    all_to_all x1, waiting for transfers between devices: 196 us -> 184 us  [body(): lax.all_to_all(own_result[chosen], 'dp', split_axis=0, concat_axis=0, til...]
    another operation x0 -> x2, local copies, waits for them, and re-layouts: none -> 8.08 us  [body(): jnp.stack([flattened] * lax.axis_size('mp'))]
    all_to_all x0 -> x1, starting transfers between devices: none -> 6.15 us  [body(): lax.all_to_all(jnp.stack([flattened] * lax.axis_size('mp')), 'mp', 0, 0)]
  transfers between devices with their start and end apart: 5 -> 5, of which waited for: 3 -> 4; matrix products, arithmetic and copies ran while one was open for 12% -> 10% of each run, Pallas kernels for 0% -> 0%
where the time goes in v1:
time: 449 us; the launch traced here: 447 us
  waiting for transfers between devices  313 us (70%)
  starting transfers between devices  39 us (9%)
  local copies, waits for them, and re-layouts  36.2 us (8%)
  matrix products  32.7 us (7%)
  between operations  14.1 us (3%)
  other arithmetic  11.8 us (3%)
    all_to_all x1, waiting for transfers between devices, body(): lax.all_to_all(own_result[chosen], 'dp', split_axis=0, concat_axis=0, til...  184 us
    all_gather x1, waiting for transfers between devices, body(): full_weight = lax.all_gather(out_weight, 'dp', axis=0, tiled=True)  79.1 us
    all_to_all x1, waiting for transfers between devices, body(): lax.all_to_all(jnp.stack([flattened] * lax.axis_size('mp')), 'mp', 0, 0)  48.2 us
    dot_general x1, matrix products, body(): jnp.dot(jnp.concatenate(lax.all_to_all(jnp.stack([flattened] * lax.axis_s...  17.9 us
    all_to_all x1, starting transfers between devices, from_everyone(): lax.all_to_all(jnp.broadcast_to(shard[None], (size, *shard.shape)), axis,...  13.1 us
    all_to_all x1, starting transfers between devices, body(): lax.all_to_all(labels, 'dp', split_axis=0, concat_axis=0, tiled=True)  10.3 us
    all_to_all x1, starting transfers between devices, body(): lax.all_to_all(own_result[chosen], 'dp', split_axis=0, concat_axis=0, til...  9.17 us
  transfers between devices with their start and end apart: 5, of which 4 were waited for; matrix products, arithmetic and copies ran while one was open for 10% of the time, Pallas kernels for 0%

profile of v1, /device:TPU:1, one launch (start us, length us, event | category | flops | bytes accessed | tf_op | source)
XLA Modules:
  0.0 447.5 jit_solution(9015103677063134631)
XLA Ops:
  7.8 13.1 %all-to-all-start = ((s32[64,1,1]{2,1,0:T(1,128)}), s32[64,1,1]{2,1,0:T(1,128)S(1)}, u32[]{:S(2)}, u32[]{:S(2)}) async-start(s32[64,1,1]{2,1,0:T(1,128)} %broadcast_in_dim.83), calls=%async_computation | async-start | bytes 65536 | tf_op jit(solution)/shard_map/all_to_all | solution.py:15
  21.0 35.8 %while.10 = (s32[]{:T(128)}, bf16[6,4,128,512]{3,2,1,0:T(8,128)(2,1)}, s32[6,4,128]{2,1,0:T(4,128)}, bf16[6,4,128,128]{3,2,1,0:T(8,128)(2,1)}, bf16[6,4,128,128]...) while((s32[]{:T(128)}, bf16[6,4,128,512]{3,2,1,0:T(8,128)(2,1)}, s32[6,4,128]{2,1,0:T(4,128)}, ...), condition=%wide.region_3.4_spmd, body=%wide.region_0.3_spmd.sunk | while | flops 137507328 | bytes 8995413 | solution.py:72
  21.0 0.7 broadcast_compare_fusion.2
  21.8 1.1 constant_dynamic-slice_fusion.2
  23.2 1.2 fusion.33
  24.6 1.3 select_convert_fusion.2
  26.1 0.8 constant_dynamic-update-slice_fusion.2
  26.9 0.7 broadcast_compare_fusion.2
  27.8 1.1 constant_dynamic-slice_fusion.2
  29.2 1.2 fusion.33
  30.6 1.3 select_convert_fusion.2
  32.1 0.8 constant_dynamic-update-slice_fusion.2
  32.9 0.7 broadcast_compare_fusion.2
  33.7 1.1 constant_dynamic-slice_fusion.2
  35.1 1.2 fusion.33
  36.5 1.3 select_convert_fusion.2
  38.0 0.8 constant_dynamic-update-slice_fusion.2
  38.9 0.7 broadcast_compare_fusion.2
  39.7 1.1 constant_dynamic-slice_fusion.2
  41.1 1.2 fusion.33
  42.5 1.3 select_convert_fusion.2
  44.0 0.8 constant_dynamic-update-slice_fusion.2
  44.8 0.7 broadcast_compare_fusion.2
  45.7 1.1 constant_dynamic-slice_fusion.2
  47.0 1.2 fusion.33
  48.5 1.3 select_convert_fusion.2
  49.9 0.8 constant_dynamic-update-slice_fusion.2
  51.6 1.1 constant_dynamic-slice_fusion.2
  53.0 1.2 fusion.33
  54.4 1.3 select_convert_fusion.2
  55.9 0.8 constant_dynamic-update-slice_fusion.2
  56.7 1.2 reduce.2
  58.0 0.7 fusion.17
  58.7 1.4 compare_select_fusion.2
  60.1 10.3 %all-to-all-start.2 = ((s32[64,1,1]{2,1,0:T(1,128)}), s32[64,1,1]{2,1,0:T(1,128)S(1)}, u32[]{:S(2)}, u32[]{:S(2)}) async-start(s32[64,1,1]{2,1,0:T(1,128)} %compare_select_fusion.2), calls=%async_computation.2 | async-start | bytes 65536 | tf_op jit(solution)/shard_map/all_to_all | solution.py:109
  70.4 0.7 fusion.19
  71.2 7.3 %gather_fusion = bf16[64,128,512]{2,1,0:T(8,128)(2,1)} fusion(bf16[24,128,512]{2,1,0:T(8,128)(2,1)} %bitcast.79, s32[1024]{0:T(1024)S(1)} %pad_clamp_fusion.1), kind=kCustom, calls=%fused_computation | custom fusion | bytes 16777472 | tf_op jit(solution)/shard_map/gather | solution.py:108
  78.5 1.2 all-to-all-done.2
  79.7 9.2 %all-to-all-start.1 = ((bf16[64,128,512]{2,1,0:T(8,128)(2,1)}), bf16[64,128,512]{2,1,0:T(8,128)(2,1)}, u32[]{:S(2)}, u32[]{:S(2)}) async-start(bf16[64,128,512]{2,1,0:T(8,128)(2,1)} %gather_fusion), calls=%async_computation.1 | async-start | bytes 16777216 | tf_op jit(solution)/shard_map/all_to_all | solution.py:108
  88.9 1.2 reduce.3
  90.4 184.3 %all-to-all-done.1 = bf16[64,128,512]{2,1,0:T(8,128)(2,1)} async-done(((bf16[64,128,512]{2,1,0:T(8,128)(2,1)}), bf16[64,128,512]{2,1,0:T(8,128)(2,1)}, u32[]{:S(2)}, u32[]{:S(2)}) %all-to-all-start.1) | async-done | bytes 8388640 | tf_op jit(solution)/shard_map/all_to_all | solution.py:108
  274.7 5.8 %gather_fusion.1 = bf16[22,128,512]{2,1,0:T(8,128)(2,1)} fusion(bf16[64,128,512]{2,1,0:T(8,128)(2,1)} %all-to-all-done.1, s32[1024]{0:T(1024)S(1)} %pad_clamp_fusion), kind=kCustom, calls=%fused_computation.1 | custom fusion | bytes 5767256 | tf_op jit(solution)/shard_map/gather | solution.py:112
  280.5 3.1 copy.40
  283.6 5.0 %stack.3 = bf16[4,2816,512]{1,2,0:T(8,128)(2,1)} broadcast(bf16[2816,512]{0,1:T(8,128)(2,1)S(1)} %copy.40), dimensions={1,2} | broadcast | bytes 14417920 | tf_op jit(solution)/shard_map/stack | solution.py:116
  288.6 6.2 %all-to-all-start.3 = ((bf16[4,2816,512]{1,2,0:T(8,128)(2,1)}), bf16[4,2816,512]{1,2,0:T(8,128)(2,1)}, u32[]{:S(2)}, u32[]{:S(2)}) async-start(bf16[4,2816,512]{1,2,0:T(8,128)(2,1)} %stack.3), calls=%async_computation.3 | async-start | bytes 23068672 | tf_op jit(solution)/shard_map/all_to_all | solution.py:116
  295.5 79.1 %all-gather.2.cloned.1.call-done = bf16[2048,1024]{1,0:T(8,128)(2,1)} async-done(((bf16[32,1024]{1,0:T(8,128)(2,1)}), bf16[2048,1024]{1,0:T(8,128)(2,1)}) %all-gather.2.cloned.1.call-update) | async-done | bytes 4194320 | tf_op jit(solution)/shard_map/all_gather | solution.py:91
  374.6 48.2 %all-to-all-done.3 = bf16[4,2816,512]{1,2,0:T(8,128)(2,1)} async-done(((bf16[4,2816,512]{1,2,0:T(8,128)(2,1)}), bf16[4,2816,512]{1,2,0:T(8,128)(2,1)}, u32[]{:S(2)}, u32[]{:S(2)}) %all-to-all-start.3) | async-done | bytes 11534368 | tf_op jit(solution)/shard_map/all_to_all | solution.py:116
  422.8 17.9 %convolution_convert_fusion = bf16[2816,1024]{1,0:T(8,128)(2,1)} fusion(bf16[2816,2048]{0,1:T(8,128)(2,1)} %bitcast.28, bf16[2048,1024]{1,0:T(8,128)(2,1)} %all-gather.2.cloned.1.call-done), kind=kOutput, calls=%fused_computation.27 | convolution fusion | flops 11814043648 | bytes 21495808 | tf_op jit(solution)/shard_map/dot_general | solution.py:114
  (41 shorter events, 7.3 us)
Async XLA Ops:
  7.8 48.9 %all-to-all-start = ((s32[64,1,1]{2,1,0:T(1,128)}), s32[64,1,1]{2,1,0:T(1,128)S(1)}, u32[]{:S(2)}, u32[]{:S(2)}) async-start(s32[64,1,1]{2,1,0:T(1,128)} %broadcast_in_dim.83), calls=%async_computation | async-start | bytes 65536 | tf_op jit(solution)/shard_map/all_to_all | solution.py:15
  60.1 19.6 %all-to-all-start.2 = ((s32[64,1,1]{2,1,0:T(1,128)}), s32[64,1,1]{2,1,0:T(1,128)S(1)}, u32[]{:S(2)}, u32[]{:S(2)}) async-start(s32[64,1,1]{2,1,0:T(1,128)} %compare_select_fusion.2), calls=%async_computation.2 | async-start | bytes 65536 | tf_op jit(solution)/shard_map/all_to_all | solution.py:109
  79.7 194.9 %all-to-all-start.1 = ((bf16[64,128,512]{2,1,0:T(8,128)(2,1)}), bf16[64,128,512]{2,1,0:T(8,128)(2,1)}, u32[]{:S(2)}, u32[]{:S(2)}) async-start(bf16[64,128,512]{2,1,0:T(8,128)(2,1)} %gather_fusion), calls=%async_computation.1 | async-start | bytes 16777216 | tf_op jit(solution)/shard_map/all_to_all | solution.py:108
  288.6 134.2 %all-to-all-start.3 = ((bf16[4,2816,512]{1,2,0:T(8,128)(2,1)}), bf16[4,2816,512]{1,2,0:T(8,128)(2,1)}, u32[]{:S(2)}, u32[]{:S(2)}) async-start(bf16[4,2816,512]{1,2,0:T(8,128)(2,1)} %stack.3), calls=%async_computation.3 | async-start | bytes 23068672 | tf_op jit(solution)/shard_map/all_to_all | solution.py:116
  294.7 79.9 %all-gather.2.cloned.1.call-start = ((), (), s32[]{:S(2)}) async-start(), calls=%async_computation.4 | async-start | bytes 4259840 | tf_op jit(solution)/shard_map/all_gather | solution.py:91
Sparse Core Ops, SparseCore 0:
  298.3 76.2 all-gather.1
